TPU v7x, 128 devices: a whole 4x4x4 slice. The times are simulated.
128 devices in a mesh: gz: 32 (over z, y, core), gy: 4 (over x).
Axes of the slice: x: 4, y: 4, z: 4, core: 2. Of those that a mesh axis runs over, the one named last changes fastest.
Arguments:
- right_side: float32 [8, 64, 256, 512], P(None, 'gz', 'gy'), may hold values from -8 to 8
- diagonal: float32 [64, 256, 512], P('gz', 'gy'), may hold values from 0.1 to 4
Outputs:
- solution: float32 [8, 64, 256, 512], P(None, 'gz', 'gy')
- hessenberg: float32 [24, 32], replicated
All inputs are finite; a program needn't handle non-finite values.
Results may differ from a plain program's by a relative error of at most 0.0003.
Values sent between devices are 32-bit elements; how exact they have to be, the bound alone decides.
A program may use at most 64 MiB of HBM per device.

v0:
```python
import functools

import jax
import jax.numpy as jnp
from jax import lax
from jax.experimental import pallas as pl
from jax.experimental.pallas import tpu as pltpu
from jax.sharding import PartitionSpec as P

MESH = pl.DeviceIdType.MESH
BLK = 8
ITERS = 3
SHIFT = 7.0
TOP = 8
Y_CHIPS = 4
CORES = 2


def iotas():
    return (
        lax.broadcasted_iota(jnp.int32, (8, 128), 0),
        lax.broadcasted_iota(jnp.int32, (8, 128), 1),
    )


def sublane(tile, at):
    return jnp.broadcast_to(tile[at : at + 1, :], (8, 128))


def lane(tile, at):
    return jnp.broadcast_to(tile[:, at : at + 1], (8, 128))


def rsqrt(value):
    guess = lax.rsqrt(value)
    return guess * (1.5 - 0.5 * value * guess * guess)


def weights_of(moments):
    sub, _ = iotas()
    one = pltpu.roll(moments, 128 - 8, 1)
    two = pltpu.roll(moments, 128 - 16, 1)
    squares = two + (2.0 * SHIFT) * one + (SHIFT * SHIFT) * moments
    right = one + SHIFT * moments
    x = [right if h == 0 else pltpu.roll(right, 128 - 8 * h, 1) for h in range(ITERS)]
    tiles = [[lane(squares, 8 * j + v) for v in range(8)] for j in range(2 * ITERS - 1)]
    rows = [[tiles[a + h][i] for h in range(ITERS)] for a in range(ITERS) for i in range(8)]
    size = 8 * ITERS
    for k in range(size):
        g, q = divmod(k, 8)
        column = rows[k]
        inverse = 1.0 / sublane(column[g], q)
        pivot = sublane(x[g], q) * inverse
        for h in range(ITERS):
            x[h] = x[h] - column[h] * pivot
        x[g] = jnp.where(sub == q, pivot, x[g])
        for r in range(k + 1, size):
            factor = sublane(column[r // 8], r % 8) * inverse
            rows[r] = [rows[r][h] - factor * column[h] for h in range(ITERS)]
            rows[r][g] = jnp.where(sub == q, factor, rows[r][g])
    return x


def hessenberg_of(moments):
    sub, lanes = iotas()
    tiles = [[lane(moments, 8 * j + v) for v in range(8)] for j in range(2 * ITERS + 1)]
    groups = ITERS + 1
    rows = [[tiles[a + h][i] for h in range(groups)] for a in range(groups) for i in range(8)]
    size = 8 * groups
    factor_of, scale_of = [], []
    for k in range(size):
        g, q = divmod(k, 8)
        scale = rsqrt(sublane(rows[k][g], q))
        column = [None if h < g else rows[k][h] * scale for h in range(groups)]
        column[g] = jnp.where(sub >= q, column[g], 0.0)
        factor_of.append(column)
        scale_of.append(scale)
        for r in range(k + 1, size):
            factor = sublane(column[r // 8], r % 8)
            for h in range(r // 8, groups):
                rows[r][h] = rows[r][h] - factor * column[h]
    x = []
    for h in range(ITERS):
        tile = jnp.zeros((8, 128), jnp.float32)
        for c in range(8 * (h + 2)):
            tile = jnp.where(lanes == c, factor_of[c][h + 1], tile)
        x.append(tile)
    for k in range(8 * ITERS):
        g, q = divmod(k, 8)
        solved = sublane(x[g], q) * scale_of[k]
        for h in range(g, ITERS):
            x[h] = x[h] - factor_of[k][h] * solved
        x[g] = jnp.where(sub == q, solved, x[g])
    return [x[h] + jnp.where(lanes == 8 * h + sub, SHIFT, 0.0) for h in range(ITERS)]


def kernel(
    n_gz, n_gy, b_ref, d_ref, out_ref, hess_ref,
    field, low_high, side_in, side_out, diag, result, spread, rows_of, moments, gathered,
    load_sem, out_sem, diag_sem, z_send, z_recv, y_send, y_recv, all_send, all_recv,
):
    gz, gy = lax.axis_index("gz"), lax.axis_index("gy")
    n_rows, n_cols = d_ref.shape[1], d_ref.shape[2]
    tiles = n_rows // 8
    core = lax.rem(gz, CORES)
    y_at = lax.rem(lax.div(gz, CORES), Y_CHIPS)
    z_at = lax.div(gz, CORES * Y_CHIPS)
    n_z = n_gz // (CORES * Y_CHIPS)
    own = pl.ds(TOP, n_rows)
    sub, lanes = iotas()

    def load(v):
        return pltpu.make_async_copy(b_ref.at[v], field.at[v, :, own, :], load_sem.at[v])

    diag_copy = pltpu.make_async_copy(d_ref, diag, diag_sem)
    load(0).start()
    load(1).start()
    diag_copy.start()
    for v in range(2, BLK):
        load(v).start()

    def first(i):
        at = lax.rem(gy * CORES + core + i, n_gy * CORES)
        return (gz - core + lax.rem(at, CORES), lax.div(at, CORES))

    def second(i):
        return (gz + (lax.rem(y_at + i, Y_CHIPS) - y_at) * CORES, gy)

    def third(i):
        return (gz + (lax.rem(z_at + i, n_z) - z_at) * CORES * Y_CHIPS, gy)

    stages = (
        (first, n_gy * CORES, gy * CORES + core, 0),
        (second, Y_CHIPS, y_at, n_gy * CORES),
        (third, n_z, z_at, n_gy * CORES + Y_CHIPS),
    )

    barrier = pltpu.get_barrier_semaphore()

    @pl.when(jnp.logical_and(core == 0, gz > 0))
    def _():
        pl.semaphore_signal(barrier, inc=1, device_id=(gz - 1, gy), device_id_type=MESH)

    @pl.when(jnp.logical_and(core == CORES - 1, gz < n_gz - 1))
    def _():
        pl.semaphore_signal(barrier, inc=1, device_id=(gz + 1, gy), device_id_type=MESH)

    count = 0
    for partner, size, _, _ in stages:
        for i in range(1, size):
            pl.semaphore_signal(barrier, inc=1, device_id=partner(i), device_id_type=MESH)
        count += size - 1

    def clear(where, buffer, side):
        @pl.when(where)
        def _():
            @pl.loop(0, ITERS * BLK)
            def _(s):
                buffer[s, side] = jnp.zeros(buffer.shape[2:], jnp.float32)

    clear(gz == 0, low_high, 0)
    clear(gz == n_gz - 1, low_high, 1)
    clear(gy == 0, side_in, 0)
    clear(gy == n_gy - 1, side_in, 1)
    moments[...] = jnp.zeros((8, 128), jnp.float32)

    off_chip = jnp.logical_or(
        jnp.logical_and(core == 0, gz > 0), jnp.logical_and(core == CORES - 1, gz < n_gz - 1)
    )

    pl.semaphore_wait(barrier, count + jnp.where(off_chip, 1, 0))

    def z_copy(s, up):
        return pltpu.make_async_remote_copy(
            src_ref=field.at[s, up, own, :],
            dst_ref=low_high.at[s, 1 - up],
            send_sem=z_send.at[s, up],
            recv_sem=z_recv.at[s, 1 - up],
            device_id=(gz + 2 * up - 1, gy),
            device_id_type=MESH,
        )

    def y_copy(s, up):
        return pltpu.make_async_remote_copy(
            src_ref=side_out.at[s, up],
            dst_ref=side_in.at[s, 1 - up],
            send_sem=y_send.at[s, up],
            recv_sem=y_recv.at[s, 1 - up],
            device_id=(gz, gy + 2 * up - 1),
            device_id_type=MESH,
        )

    has_z = (gz > 0, gz < n_gz - 1)
    has_y = (gy > 0, gy < n_gy - 1)

    def send(s):
        for up in (0, 1):

            @pl.when(has_z[up])
            def _(up=up):
                z_copy(s, up).start()

        for layer in (0, 1):
            side_out[s, 0, layer] = field[s, layer, TOP : TOP + 1, :]
            side_out[s, 1, layer] = field[s, layer, TOP + n_rows - 1 : TOP + n_rows, :]
        for up in (0, 1):

            @pl.when(has_y[up])
            def _(up=up):
                y_copy(s, up).start()

    def arrive(s):
        for up in (0, 1):

            @pl.when(has_z[up])
            def _(up=up):
                z_copy(s, 1 - up).wait_recv()

            @pl.when(has_y[up])
            def _(up=up):
                y_copy(s, 1 - up).wait_recv()

        for layer in (0, 1):
            field[s, layer, TOP - 1 : TOP, :] = side_in[s, 0, layer]
            field[s, layer, TOP + n_rows : TOP + n_rows + 1, :] = side_in[s, 1, layer]

    lane_of_row = lax.broadcasted_iota(jnp.int32, (8, n_cols), 1)

    def apply(s):
        f = s - BLK
        for layer in (0, 1):
            for t in range(tiles):
                low = TOP + 8 * t
                here = field[f, layer, low : low + 8, :]
                beside = field[f, layer, low - 1 : low + 7, :] + field[f, layer, low + 1 : low + 9, :]
                other = field[f, 1 - layer, low : low + 8, :]
                beside = beside + (other + low_high[f, layer, 8 * t : 8 * t + 8, :])
                left = jnp.where(lane_of_row == 0, 0.0, pltpu.roll(here, 1, 1))
                right = jnp.where(lane_of_row == n_cols - 1, 0.0, pltpu.roll(here, n_cols - 1, 1))
                field[s, layer, low : low + 8, :] = diag[layer, 8 * t : 8 * t + 8, :] * here - (
                    beside + (left + right)
                )

    def fold(row):
        total = row[:, :128]
        for at in range(128, n_cols, 128):
            total = total + row[:, at : at + 128]
        return jnp.sum(total, axis=0, keepdims=True)

    def products(s, v, others):
        @pl.loop(0, v + 1)
        def _(u):
            totals = [jnp.zeros((8, n_cols), jnp.float32) for _ in others]
            for layer in (0, 1):
                for t in range(tiles):
                    low = TOP + 8 * t
                    here = field[s, layer, low : low + 8, :]
                    totals = [
                        total + here * field[u + other, layer, low : low + 8, :]
                        for total, other in zip(totals, others)
                    ]
            for at, total in enumerate(totals):
                rows_of[at, pl.ds(u, 1), :] = fold(total)

    def place(at, j, v):
        values = jnp.sum(rows_of[at], axis=1, keepdims=True)
        values = jnp.where(sub <= v, values, 0.0)
        new = jnp.where(lanes == j * 8 + v, values, 0.0)
        turned = jnp.where(jnp.logical_and(lanes == j * 8 + sub, sub < v), values, 0.0)
        turned = jnp.sum(turned, axis=0, keepdims=True)
        moments[...] = moments[...] + (new + jnp.where(sub == v, turned, 0.0))

    rows_of[...] = jnp.zeros(rows_of.shape, jnp.float32)

    @pl.loop(0, BLK)
    def _(v):
        load(v).wait()
        send(v)
        products(v, v, (0,))
        place(0, 0, v)

    diag_copy.wait()
    diag[...] = diag[...] + (6.0 - SHIFT)

    @pl.loop(BLK, (ITERS + 1) * BLK)
    def _(s):
        k, v = lax.div(s, BLK), lax.rem(s, BLK)
        arrive(s - BLK)
        apply(s)

        @pl.when(s < ITERS * BLK)
        def _():
            send(s)

        products(s, v, (k * BLK - BLK, k * BLK))
        place(0, 2 * k - 1, v)
        place(1, 2 * k, v)

    total = moments[...]
    for at, (partner, size, me, base) in enumerate(stages):
        gathered[base + me] = total

        def copy(i):
            return pltpu.make_async_remote_copy(
                src_ref=gathered.at[base + me],
                dst_ref=gathered.at[base + me],
                send_sem=all_send.at[base + i],
                recv_sem=all_recv.at[base + i],
                device_id=partner(i),
                device_id_type=MESH,
            )

        for i in range(1, size):
            copy(i).start()
        for i in range(1, size):
            copy(i).wait_recv()
        total = gathered[base]
        for i in range(1, size):
            total = total + gathered[base + i]
        for i in range(1, size):
            copy(i).wait_send()

    weights = weights_of(total)
    for h in range(ITERS):
        for i in range(BLK):
            spread[i, 8 * h : 8 * h + 8, :] = lane(weights[h], i)
    for h, tile in enumerate(hessenberg_of(total)):
        hess_ref[8 * h : 8 * h + 8, :] = tile[:, : hess_ref.shape[1]]

    def store(i):
        return pltpu.make_async_copy(result.at[i], out_ref.at[i], out_sem.at[i])

    @pl.loop(0, BLK)
    def _(i):
        factors = [
            jnp.broadcast_to(spread[i, j : j + 1, :], (8, 128)) for j in range(ITERS * BLK)
        ]
        for layer in (0, 1):

            @pl.loop(0, tiles)
            def _(t):
                low = pl.multiple_of(8 * t, 8)
                for at in range(0, n_cols, 128):
                    parts = [None] * 4
                    for j in range(ITERS * BLK):
                        term = factors[j] * field[j, layer, pl.ds(TOP + low, 8), at : at + 128]
                        parts[j % 4] = term if parts[j % 4] is None else parts[j % 4] + term
                    result[i, layer, pl.ds(low, 8), at : at + 128] = (parts[0] + parts[1]) + (
                        parts[2] + parts[3]
                    )

        store(i).start()

    @pl.loop(0, ITERS * BLK)
    def _(s):
        for up in (0, 1):

            @pl.when(has_z[up])
            def _(up=up):
                z_copy(s, up).wait_send()

            @pl.when(has_y[up])
            def _(up=up):
                y_copy(s, up).wait_send()

    @pl.loop(0, BLK)
    def _(i):
        store(i).wait()


def solution(mesh):
    n_gz, n_gy = mesh.shape["gz"], mesh.shape["gy"]
    n_z = n_gz // (CORES * Y_CHIPS)
    partners = n_gy * CORES + Y_CHIPS + n_z

    def body(right_side, diagonal):
        layers, n_rows, n_cols = diagonal.shape
        powers = ITERS * BLK
        vmem = lambda *shape: pltpu.VMEM(shape, jnp.float32)
        dma = pltpu.SemaphoreType.DMA
        return pl.pallas_call(
            functools.partial(kernel, n_gz, n_gy),
            out_shape=(
                jax.ShapeDtypeStruct(right_side.shape, jnp.float32),
                jax.ShapeDtypeStruct((powers, powers + BLK), jnp.float32),
            ),
            in_specs=[pl.BlockSpec(memory_space=pltpu.HBM)] * 2,
            out_specs=(
                pl.BlockSpec(memory_space=pltpu.HBM),
                pl.BlockSpec(memory_space=pltpu.VMEM),
            ),
            scratch_shapes=[
                vmem(powers + BLK, layers, n_rows + 2 * TOP, n_cols),
                vmem(powers, 2, n_rows, n_cols),
                vmem(powers, 2, layers, 1, n_cols),
                vmem(powers, 2, layers, 1, n_cols),
                vmem(layers, n_rows, n_cols),
                vmem(BLK, layers, n_rows, n_cols),
                vmem(BLK, powers, 128),
                vmem(2, 8, 128),
                vmem(8, 128),
                vmem(partners, 8, 128),
                dma((BLK,)),
                dma((BLK,)),
                dma,
                dma((powers, 2)),
                dma((powers, 2)),
                dma((powers, 2)),
                dma((powers, 2)),
                dma((partners,)),
                dma((partners,)),
            ],
            compiler_params=pltpu.CompilerParams(collective_id=0, has_side_effects=True),
            name="block_gmres",
        )(right_side, diagonal)

    placed = (P(None, "gz", "gy", None), P("gz", "gy", None))
    return jax.shard_map(
        body, mesh=mesh, in_specs=placed, out_specs=(placed[0], P()), check_vma=False
    )
```

profile of v0, /device:TPU:1, one launch (start us, length us, event | category | flops | bytes accessed | tf_op | source)
XLA Modules:
  0.0 68.2 jit_solution(4614212468530636458)
XLA Ops:
  0.6 63.8 %block_gmres.1 = (f32[8,2,64,512]{3,2,1,0:T(8,128)}, f32[24,32]{1,0:T(8,128)}) custom-call(f32[8,2,64,512]{3,2,1,0:T(8,128)} %b_ref.1, f32[2,64,512]{2,1,0:T(8,128)} %d_ref.1), custom_call_target="tpu_custom_call" | custom-call | tf_op jit(solution)/shard_map/block_gmres/pallas_call | solution.py:381
  64.5 0.0 copy-start
  64.5 3.1 %copy.6 = f32[8,2,64,512]{3,2,1,0:T(8,128)} copy(f32[8,2,64,512]{3,2,1,0:T(8,128)} %get-tuple-element.4) | data formatting | bytes 4194304
  67.6 0.0 copy-done
  67.6 0.6 copy.7
Async XLA Ops:
  64.5 3.2 %copy-start = (f32[24,32]{1,0:T(8,128)S(1)}, f32[24,32]{1,0:T(8,128)}, u32[]{:S(2)}) copy-start(f32[24,32]{1,0:T(8,128)} %get-tuple-element.5) | copy-start | bytes 9220
where the time goes:
time: 69.1 us; the launch traced here: 68.2 us
  Pallas kernels  63.8 us (92%)
  local copies, waits for them, and re-layouts  3.75 us (5%)
    pallas_call x1, Pallas kernels, body(): pl.pallas_call(functools.partial(kernel, n_gz, n_gy), out_shape=(jax.Shap...  63.8 us
    unnamed x4, local copies, waits for them, and re-layouts  3.75 us

commit v1 on v0

--- a/solution.py
+++ b/solution.py
@@ -95,9 +95,9 @@
 
 
 def kernel(
-    n_gz, n_gy, b_ref, d_ref, out_ref, hess_ref,
-    field, low_high, side_in, side_out, diag, result, spread, rows_of, moments, gathered,
-    load_sem, out_sem, diag_sem, z_send, z_recv, y_send, y_recv, all_send, all_recv,
+    n_gz, n_gy, b_ref, d_ref, high_ref, low_ref, mix_ref, hess_ref,
+    field, low_high, side_in, side_out, diag, rows_of, moments, gathered,
+    load_sem, diag_sem, z_send, z_recv, y_send, y_recv, all_send, all_recv, ready,
 ):
     gz, gy = lax.axis_index("gz"), lax.axis_index("gy")
     n_rows, n_cols = d_ref.shape[1], d_ref.shape[2]
@@ -119,20 +119,30 @@
     for v in range(2, BLK):
         load(v).start()
 
-    def first(i):
+    def x_core(i):
         at = lax.rem(gy * CORES + core + i, n_gy * CORES)
         return (gz - core + lax.rem(at, CORES), lax.div(at, CORES))
 
+    def along_y(i):
+        return (gz + (lax.rem(y_at + i, Y_CHIPS) - y_at) * CORES, gy)
+
+    def along_z(i):
+        return (gz + (lax.rem(z_at + i, n_z) - z_at) * CORES * Y_CHIPS, gy)
+
+    def first(i):
+        at = lax.rem(y_at * n_gy + gy + i, Y_CHIPS * n_gy)
+        return (gz + (lax.div(at, n_gy) - y_at) * CORES, lax.rem(at, n_gy))
+
     def second(i):
-        return (gz + (lax.rem(y_at + i, Y_CHIPS) - y_at) * CORES, gy)
-
-    def third(i):
-        return (gz + (lax.rem(z_at + i, n_z) - z_at) * CORES * Y_CHIPS, gy)
+        at = lax.rem(z_at * CORES + core + i, n_z * CORES)
+        return (
+            gz + (lax.div(at, CORES) - z_at) * CORES * Y_CHIPS + lax.rem(at, CORES) - core,
+            gy,
+        )
 
     stages = (
-        (first, n_gy * CORES, gy * CORES + core, 0),
-        (second, Y_CHIPS, y_at, n_gy * CORES),
-        (third, n_z, z_at, n_gy * CORES + Y_CHIPS),
+        (first, Y_CHIPS * n_gy, y_at * n_gy + gy, 0),
+        (second, n_z * CORES, z_at * CORES + core, Y_CHIPS * n_gy),
     )
 
     barrier = pltpu.get_barrier_semaphore()
@@ -146,7 +156,7 @@
         pl.semaphore_signal(barrier, inc=1, device_id=(gz + 1, gy), device_id_type=MESH)
 
     count = 0
-    for partner, size, _, _ in stages:
+    for partner, size in ((along_z, n_z), (along_y, Y_CHIPS), (x_core, n_gy * CORES)):
         for i in range(1, size):
             pl.semaphore_signal(barrier, inc=1, device_id=partner(i), device_id_type=MESH)
         count += size - 1
@@ -270,12 +280,30 @@
         turned = jnp.sum(turned, axis=0, keepdims=True)
         moments[...] = moments[...] + (new + jnp.where(sub == v, turned, 0.0))
 
+    def split(k, part):
+        for layer in (0, 1):
+            low = pl.multiple_of(TOP + 8 * part, 8)
+            values = field[pl.ds(k * BLK, BLK), layer, pl.ds(low, 8), :].reshape(8 * BLK, n_cols)
+            high = values.astype(jnp.bfloat16)
+            to = pl.ds(pl.multiple_of(k * (8 * BLK), 8 * BLK), 8 * BLK)
+            high_ref[layer * tiles + part, to, :] = high
+            low_ref[layer * tiles + part, to, :] = (values - high.astype(jnp.float32)).astype(
+                jnp.bfloat16
+            )
+
     rows_of[...] = jnp.zeros(rows_of.shape, jnp.float32)
 
     @pl.loop(0, BLK)
     def _(v):
         load(v).wait()
         send(v)
+
+    for partner, size in ((along_z, n_z), (along_y, Y_CHIPS)):
+        for i in range(1, size):
+            pl.semaphore_signal(ready, inc=1, device_id=partner(i), device_id_type=MESH)
+
+    @pl.loop(0, BLK)
+    def _(v):
         products(v, v, (0,))
         place(0, 0, v)
 
@@ -296,60 +324,57 @@
         place(0, 2 * k - 1, v)
         place(1, 2 * k, v)
 
+        split(k - 1, v)
+
+    pl.semaphore_wait(ready, (n_z - 1) + (Y_CHIPS - 1))
+
+    def copy(stage, i):
+        partner, _, me, base = stage
+        return pltpu.make_async_remote_copy(
+            src_ref=gathered.at[base + me],
+            dst_ref=gathered.at[base + me],
+            send_sem=all_send.at[base + i],
+            recv_sem=all_recv.at[base + i],
+            device_id=partner(i),
+            device_id_type=MESH,
+        )
+
     total = moments[...]
-    for at, (partner, size, me, base) in enumerate(stages):
+    for stage in stages:
+        _, size, me, base = stage
         gathered[base + me] = total
-
-        def copy(i):
-            return pltpu.make_async_remote_copy(
-                src_ref=gathered.at[base + me],
-                dst_ref=gathered.at[base + me],
-                send_sem=all_send.at[base + i],
-                recv_sem=all_recv.at[base + i],
-                device_id=partner(i),
-                device_id_type=MESH,
-            )
-
         for i in range(1, size):
-            copy(i).start()
+            copy(stage, i).start()
         for i in range(1, size):
-            copy(i).wait_recv()
+            copy(stage, i).wait_recv()
         total = gathered[base]
         for i in range(1, size):
             total = total + gathered[base + i]
-        for i in range(1, size):
-            copy(i).wait_send()
 
     weights = weights_of(total)
-    for h in range(ITERS):
-        for i in range(BLK):
-            spread[i, 8 * h : 8 * h + 8, :] = lane(weights[h], i)
+    eighth, within = lax.div(lanes, 8), lax.rem(lanes, 8)
+    for i in range(0, BLK, 2):
+        wide = []
+        for at in (i, i + 1):
+            column = [lane(weights[h], at) for h in range(ITERS)]
+            front = jnp.where(eighth == sub, column[0], 0.0) + jnp.where(
+                eighth == sub + 8, column[1], 0.0
+            )
+            back = jnp.where(eighth == sub, column[2], 0.0)
+            wide.append(
+                [
+                    jnp.where(within == sub, jnp.sum(part, axis=0, keepdims=True), 0.0)
+                    for part in (front, back)
+                ]
+            )
+        for part, (start, stop) in enumerate(((0, 128), (128, 8 * BLK * ITERS))):
+            both = jnp.concatenate([wide[0][part], wide[1][part]], axis=0)
+            high = both.astype(jnp.bfloat16)
+            low = (both - high.astype(jnp.float32)).astype(jnp.bfloat16)
+            mix_ref[8 * i : 8 * i + 16, start:stop] = high[:, : stop - start]
+            mix_ref[64 + 8 * i : 64 + 8 * i + 16, start:stop] = low[:, : stop - start]
     for h, tile in enumerate(hessenberg_of(total)):
         hess_ref[8 * h : 8 * h + 8, :] = tile[:, : hess_ref.shape[1]]
-
-    def store(i):
-        return pltpu.make_async_copy(result.at[i], out_ref.at[i], out_sem.at[i])
-
-    @pl.loop(0, BLK)
-    def _(i):
-        factors = [
-            jnp.broadcast_to(spread[i, j : j + 1, :], (8, 128)) for j in range(ITERS * BLK)
-        ]
-        for layer in (0, 1):
-
-            @pl.loop(0, tiles)
-            def _(t):
-                low = pl.multiple_of(8 * t, 8)
-                for at in range(0, n_cols, 128):
-                    parts = [None] * 4
-                    for j in range(ITERS * BLK):
-                        term = factors[j] * field[j, layer, pl.ds(TOP + low, 8), at : at + 128]
-                        parts[j % 4] = term if parts[j % 4] is None else parts[j % 4] + term
-                    result[i, layer, pl.ds(low, 8), at : at + 128] = (parts[0] + parts[1]) + (
-                        parts[2] + parts[3]
-                    )
-
-        store(i).start()
 
     @pl.loop(0, ITERS * BLK)
     def _(s):
@@ -363,44 +388,62 @@
             def _(up=up):
                 y_copy(s, up).wait_send()
 
-    @pl.loop(0, BLK)
-    def _(i):
-        store(i).wait()
+    for stage in stages:
+        for i in range(1, stage[1]):
+            copy(stage, i).wait_send()
+
+
+def combine(high_ref, low_ref, mix_ref, h_ref, out_ref, hess_ref, result, out_sem):
+    hess_ref[...] = h_ref[...]
+    tiles = high_ref.shape[0] // 2
+
+    def store(n):
+        where = (slice(None), n // tiles, pl.ds(8 * (n % tiles), 8))
+        return pltpu.make_async_copy(result.at[where], out_ref.at[where], out_sem.at[n])
+
+    for n in range(2 * tiles):
+        both = jnp.dot(mix_ref[...], high_ref[n], preferred_element_type=jnp.float32)
+        rest = jnp.dot(mix_ref[:64], low_ref[n], preferred_element_type=jnp.float32)
+        total = both[:64] + (both[64:] + rest)
+        result[:, n // tiles, 8 * (n % tiles) : 8 * (n % tiles) + 8, :] = total.reshape(
+            BLK, 8, total.shape[1]
+        )
+        store(n).start()
+    for n in range(2 * tiles):
+        store(n).wait()
 
 
 def solution(mesh):
     n_gz, n_gy = mesh.shape["gz"], mesh.shape["gy"]
     n_z = n_gz // (CORES * Y_CHIPS)
-    partners = n_gy * CORES + Y_CHIPS + n_z
+    partners = n_gy * Y_CHIPS + n_z * CORES
 
     def body(right_side, diagonal):
         layers, n_rows, n_cols = diagonal.shape
         powers = ITERS * BLK
+        pieces = layers * n_rows // 8
         vmem = lambda *shape: pltpu.VMEM(shape, jnp.float32)
         dma = pltpu.SemaphoreType.DMA
-        return pl.pallas_call(
+        whole = pl.BlockSpec(memory_space=pltpu.VMEM)
+        high, low, mix, hessenberg = pl.pallas_call(
             functools.partial(kernel, n_gz, n_gy),
             out_shape=(
-                jax.ShapeDtypeStruct(right_side.shape, jnp.float32),
+                jax.ShapeDtypeStruct((pieces, 8 * powers, n_cols), jnp.bfloat16),
+                jax.ShapeDtypeStruct((pieces, 8 * powers, n_cols), jnp.bfloat16),
+                jax.ShapeDtypeStruct((16 * BLK, 8 * powers), jnp.bfloat16),
                 jax.ShapeDtypeStruct((powers, powers + BLK), jnp.float32),
             ),
             in_specs=[pl.BlockSpec(memory_space=pltpu.HBM)] * 2,
-            out_specs=(
-                pl.BlockSpec(memory_space=pltpu.HBM),
-                pl.BlockSpec(memory_space=pltpu.VMEM),
-            ),
+            out_specs=(whole,) * 4,
             scratch_shapes=[
                 vmem(powers + BLK, layers, n_rows + 2 * TOP, n_cols),
                 vmem(powers, 2, n_rows, n_cols),
                 vmem(powers, 2, layers, 1, n_cols),
                 vmem(powers, 2, layers, 1, n_cols),
                 vmem(layers, n_rows, n_cols),
-                vmem(BLK, layers, n_rows, n_cols),
-                vmem(BLK, powers, 128),
                 vmem(2, 8, 128),
                 vmem(8, 128),
                 vmem(partners, 8, 128),
-                dma((BLK,)),
                 dma((BLK,)),
                 dma,
                 dma((powers, 2)),
@@ -409,10 +452,25 @@
                 dma((powers, 2)),
                 dma((partners,)),
                 dma((partners,)),
+                pltpu.SemaphoreType.REGULAR,
             ],
-            compiler_params=pltpu.CompilerParams(collective_id=0, has_side_effects=True),
+            compiler_params=pltpu.CompilerParams(
+                collective_id=0, has_side_effects=True, vmem_limit_bytes=28 << 20
+            ),
             name="block_gmres",
-        )(right_side, diagonal)
+        )(*(pltpu.with_memory_space_constraint(a, pltpu.HBM) for a in (right_side, diagonal)))
+        return pl.pallas_call(
+            combine,
+            out_shape=(
+                jax.ShapeDtypeStruct(right_side.shape, jnp.float32),
+                jax.ShapeDtypeStruct(hessenberg.shape, jnp.float32),
+            ),
+            in_specs=[whole] * 4,
+            out_specs=(pl.BlockSpec(memory_space=pltpu.HBM), whole),
+            scratch_shapes=[vmem(*right_side.shape), dma((pieces,))],
+            compiler_params=pltpu.CompilerParams(vmem_limit_bytes=12 << 20),
+            name="combine",
+        )(high, low, mix, hessenberg)
 
     placed = (P(None, "gz", "gy", None), P("gz", "gy", None))
     return jax.shard_map(

time: 69.1 us -> 59.8 us (0.87); the launches traced: 68.2 us -> 59.7 us
  Pallas kernels: 63.8 us -> 59.1 us
  local copies, waits for them, and re-layouts: 3.75 us -> 0 us
    pallas_call x1, Pallas kernels: 63.8 us -> 56.4 us  [body(): pl.pallas_call(functools.partial(kernel, n_gz, n_gy), out_shape=(jax.Shap...]
    unnamed x4 -> x0, local copies, waits for them, and re-layouts: 3.75 us -> none
    pallas_call x0 -> x1, Pallas kernels: none -> 2.7 us  [body(): pl.pallas_call(combine, out_shape=(jax.ShapeDtypeStruct(right_side.shape,...]
where the time goes in v1:
time: 59.8 us; the launch traced here: 59.7 us
  Pallas kernels  59.1 us (99%)
  between operations  0.64 us (1%)
    pallas_call x1, Pallas kernels, body(): pl.pallas_call(functools.partial(kernel, n_gz, n_gy), out_shape=(jax.Shap...  56.4 us
    pallas_call x1, Pallas kernels, body(): pl.pallas_call(combine, out_shape=(jax.ShapeDtypeStruct(right_side.shape,...  2.7 us

profile of v1, /device:TPU:1, one launch (start us, length us, event | category | flops | bytes accessed | tf_op | source)
XLA Modules:
  0.0 59.7 jit_solution(14170578681020074390)
XLA Ops:
  0.6 56.4 %block_gmres.1 = (bf16[16,192,512]{2,1,0:T(8,128)(2,1)S(1)}, bf16[16,192,512]{2,1,0:T(8,128)(2,1)S(1)}, bf16[128,192]{1,0:T(8,128)(2,1)S(1)}, f32[24,32]{1,0:T(8,128)S(1)}) custom-call(f32[8,2,64,512]{3,2,1,0:T(8,128)} %b_ref.1, f32[2,64,512]{2,1,0:T(8,128)} %d_ref.1), custom_call_target="tpu_custom_call" | custom-call | tf_op jit(solution)/shard_map/block_gmres/pallas_call | solution.py:428
  57.0 2.7 %combine.1 = (f32[8,2,64,512]{3,2,1,0:T(8,128)}, f32[24,32]{1,0:T(8,128)}) custom-call(bf16[16,192,512]{2,1,0:T(8,128)(2,1)S(1)} %get-tuple-element.6.high_ref, bf16[16,192,512]{2,1,0:T(8,128)(2,1)S(1)} %get-tuple-element.7.low_ref, bf16[128,192]{1,0:T(8,128)(2,1)S(1)} %get-tuple-element.8.mix_ref, f32[24,32]{1,0:T(8,128)S(1)} %get-tuple-element.9.h_ref), custom_call_target="tpu_custom_call" | custom-call | tf_op jit(solution)/shard_map/combine/pallas_call | solution.py:462

commit v2 on v1

--- a/solution.py
+++ b/solution.py
@@ -95,7 +95,7 @@
 
 
 def kernel(
-    n_gz, n_gy, b_ref, d_ref, high_ref, low_ref, mix_ref, hess_ref,
+    n_gz, n_gy, b_ref, d_ref, high_ref, low_ref, mix_ref, sum_ref,
     field, low_high, side_in, side_out, diag, rows_of, moments, gathered,
     load_sem, diag_sem, z_send, z_recv, y_send, y_recv, all_send, all_recv, ready,
 ):
@@ -106,6 +106,7 @@
     y_at = lax.rem(lax.div(gz, CORES), Y_CHIPS)
     z_at = lax.div(gz, CORES * Y_CHIPS)
     n_z = n_gz // (CORES * Y_CHIPS)
+    fast = 1 - core
     own = pl.ds(TOP, n_rows)
     sub, lanes = iotas()
 
@@ -119,47 +120,40 @@
     for v in range(2, BLK):
         load(v).start()
 
-    def x_core(i):
-        at = lax.rem(gy * CORES + core + i, n_gy * CORES)
-        return (gz - core + lax.rem(at, CORES), lax.div(at, CORES))
-
-    def along_y(i):
-        return (gz + (lax.rem(y_at + i, Y_CHIPS) - y_at) * CORES, gy)
-
-    def along_z(i):
-        return (gz + (lax.rem(z_at + i, n_z) - z_at) * CORES * Y_CHIPS, gy)
+    def around(at, i, size):
+        return at + i if i == 0 else jnp.where(at + i >= size, at + (i - size), at + i)
 
     def first(i):
-        at = lax.rem(y_at * n_gy + gy + i, Y_CHIPS * n_gy)
-        return (gz + (lax.div(at, n_gy) - y_at) * CORES, lax.rem(at, n_gy))
+        return (gz + (around(y_at, i // n_gy, Y_CHIPS) - y_at) * CORES, around(gy, i % n_gy, n_gy))
 
     def second(i):
-        at = lax.rem(z_at * CORES + core + i, n_z * CORES)
-        return (
-            gz + (lax.div(at, CORES) - z_at) * CORES * Y_CHIPS + lax.rem(at, CORES) - core,
-            gy,
-        )
+        to = (around(z_at, i // CORES, n_z) - z_at) * CORES * Y_CHIPS
+        return (gz + to + around(core, i % CORES, CORES) - core, gy)
 
     stages = (
         (first, Y_CHIPS * n_gy, y_at * n_gy + gy, 0),
         (second, n_z * CORES, z_at * CORES + core, Y_CHIPS * n_gy),
     )
 
+    def tell(semaphore, gz_step, gy_step):
+        count = 0
+        for sign in (-1, 1):
+            to_gz, to_gy = gz + sign * gz_step, gy + sign * gy_step
+            there = jnp.logical_and(
+                jnp.logical_and(to_gz >= 0, to_gz < n_gz), jnp.logical_and(to_gy >= 0, to_gy < n_gy)
+            )
+
+            @pl.when(there)
+            def _(to_gz=to_gz, to_gy=to_gy):
+                pl.semaphore_signal(
+                    semaphore, inc=1, device_id=(to_gz, to_gy), device_id_type=MESH
+                )
+
+            count += jnp.where(there, 1, 0)
+        return count
+
     barrier = pltpu.get_barrier_semaphore()
-
-    @pl.when(jnp.logical_and(core == 0, gz > 0))
-    def _():
-        pl.semaphore_signal(barrier, inc=1, device_id=(gz - 1, gy), device_id_type=MESH)
-
-    @pl.when(jnp.logical_and(core == CORES - 1, gz < n_gz - 1))
-    def _():
-        pl.semaphore_signal(barrier, inc=1, device_id=(gz + 1, gy), device_id_type=MESH)
-
-    count = 0
-    for partner, size in ((along_z, n_z), (along_y, Y_CHIPS), (x_core, n_gy * CORES)):
-        for i in range(1, size):
-            pl.semaphore_signal(barrier, inc=1, device_id=partner(i), device_id_type=MESH)
-        count += size - 1
+    expected = tell(barrier, 1, 0) + tell(barrier, 0, 1)
 
     def clear(where, buffer, side):
         @pl.when(where)
@@ -174,11 +168,27 @@
     clear(gy == n_gy - 1, side_in, 1)
     moments[...] = jnp.zeros((8, 128), jnp.float32)
 
-    off_chip = jnp.logical_or(
-        jnp.logical_and(core == 0, gz > 0), jnp.logical_and(core == CORES - 1, gz < n_gz - 1)
-    )
-
-    pl.semaphore_wait(barrier, count + jnp.where(off_chip, 1, 0))
+    off_chip = jnp.where(core == 0, gz > 0, gz < n_gz - 1)
+
+    pl.semaphore_wait(barrier, expected)
+
+    rounds = []
+    step = 1
+    while step < n_gz:
+        rounds.append((step, 0))
+        step *= 2
+    rounds += [(0, 1)] * (n_gy - 1)
+
+    def knows(r):
+        gz_step, gy_step = rounds[r]
+        count = 0
+        for sign in (-1, 1):
+            to_gz, to_gy = gz + sign * gz_step, gy + sign * gy_step
+            there = jnp.logical_and(
+                jnp.logical_and(to_gz >= 0, to_gz < n_gz), jnp.logical_and(to_gy >= 0, to_gy < n_gy)
+            )
+            count += jnp.where(there, 1, 0)
+        pl.semaphore_wait(ready.at[r], count)
 
     def z_copy(s, up):
         return pltpu.make_async_remote_copy(
@@ -200,16 +210,18 @@
             device_id_type=MESH,
         )
 
-    has_z = (gz > 0, gz < n_gz - 1)
     has_y = (gy > 0, gy < n_gy - 1)
 
-    def send(s):
-        for up in (0, 1):
-
-            @pl.when(has_z[up])
-            def _(up=up):
-                z_copy(s, up).start()
-
+    def send_z(s, layer):
+        if layer is fast:
+            z_copy(s, fast).start()
+        else:
+
+            @pl.when(off_chip)
+            def _():
+                z_copy(s, core).start()
+
+    def send_y(s):
         for layer in (0, 1):
             side_out[s, 0, layer] = field[s, layer, TOP : TOP + 1, :]
             side_out[s, 1, layer] = field[s, layer, TOP + n_rows - 1 : TOP + n_rows, :]
@@ -219,12 +231,8 @@
             def _(up=up):
                 y_copy(s, up).start()
 
-    def arrive(s):
+    def arrive_y(s):
         for up in (0, 1):
-
-            @pl.when(has_z[up])
-            def _(up=up):
-                z_copy(s, 1 - up).wait_recv()
 
             @pl.when(has_y[up])
             def _(up=up):
@@ -234,22 +242,30 @@
             field[s, layer, TOP - 1 : TOP, :] = side_in[s, 0, layer]
             field[s, layer, TOP + n_rows : TOP + n_rows + 1, :] = side_in[s, 1, layer]
 
+    def arrive_z(s, layer):
+        if layer is fast:
+            z_copy(s, core).wait_recv()
+        else:
+
+            @pl.when(off_chip)
+            def _():
+                z_copy(s, fast).wait_recv()
+
     lane_of_row = lax.broadcasted_iota(jnp.int32, (8, n_cols), 1)
 
-    def apply(s):
+    def apply(s, layer):
         f = s - BLK
-        for layer in (0, 1):
-            for t in range(tiles):
-                low = TOP + 8 * t
-                here = field[f, layer, low : low + 8, :]
-                beside = field[f, layer, low - 1 : low + 7, :] + field[f, layer, low + 1 : low + 9, :]
-                other = field[f, 1 - layer, low : low + 8, :]
-                beside = beside + (other + low_high[f, layer, 8 * t : 8 * t + 8, :])
-                left = jnp.where(lane_of_row == 0, 0.0, pltpu.roll(here, 1, 1))
-                right = jnp.where(lane_of_row == n_cols - 1, 0.0, pltpu.roll(here, n_cols - 1, 1))
-                field[s, layer, low : low + 8, :] = diag[layer, 8 * t : 8 * t + 8, :] * here - (
-                    beside + (left + right)
-                )
+        for t in range(tiles):
+            low = TOP + 8 * t
+            here = field[f, layer, low : low + 8, :]
+            beside = field[f, layer, low - 1 : low + 7, :] + field[f, layer, low + 1 : low + 9, :]
+            other = field[f, 1 - layer, low : low + 8, :]
+            beside = beside + (other + low_high[f, layer, 8 * t : 8 * t + 8, :])
+            left = jnp.where(lane_of_row == 0, 0.0, pltpu.roll(here, 1, 1))
+            right = jnp.where(lane_of_row == n_cols - 1, 0.0, pltpu.roll(here, n_cols - 1, 1))
+            field[s, layer, low : low + 8, :] = diag[layer, 8 * t : 8 * t + 8, :] * here - (
+                beside + (left + right)
+            )
 
     def fold(row):
         total = row[:, :128]
@@ -257,11 +273,11 @@
             total = total + row[:, at : at + 128]
         return jnp.sum(total, axis=0, keepdims=True)
 
-    def products(s, v, others):
+    def products(s, v, others, layers, more=False):
         @pl.loop(0, v + 1)
         def _(u):
             totals = [jnp.zeros((8, n_cols), jnp.float32) for _ in others]
-            for layer in (0, 1):
+            for layer in layers:
                 for t in range(tiles):
                     low = TOP + 8 * t
                     here = field[s, layer, low : low + 8, :]
@@ -270,7 +286,10 @@
                         for total, other in zip(totals, others)
                     ]
             for at, total in enumerate(totals):
-                rows_of[at, pl.ds(u, 1), :] = fold(total)
+                new = fold(total)
+                if more:
+                    new = new + rows_of[at, pl.ds(u, 1), :]
+                rows_of[at, pl.ds(u, 1), :] = new
 
     def place(at, j, v):
         values = jnp.sum(rows_of[at], axis=1, keepdims=True)
@@ -296,15 +315,13 @@
     @pl.loop(0, BLK)
     def _(v):
         load(v).wait()
-        send(v)
-
-    for partner, size in ((along_z, n_z), (along_y, Y_CHIPS)):
-        for i in range(1, size):
-            pl.semaphore_signal(ready, inc=1, device_id=partner(i), device_id_type=MESH)
+        send_z(v, core)
+        send_z(v, fast)
+        send_y(v)
 
     @pl.loop(0, BLK)
     def _(v):
-        products(v, v, (0,))
+        products(v, v, (0,), (0, 1))
         place(0, 0, v)
 
     diag_copy.wait()
@@ -313,20 +330,37 @@
     @pl.loop(BLK, (ITERS + 1) * BLK)
     def _(s):
         k, v = lax.div(s, BLK), lax.rem(s, BLK)
-        arrive(s - BLK)
-        apply(s)
+        others = (k * BLK - BLK, k * BLK)
+        for r in range(len(rounds) + 1):
+
+            @pl.when(s == BLK + r)
+            def _(r=r):
+                if r > 0:
+                    knows(r - 1)
+                if r < len(rounds):
+                    tell(ready.at[r], *rounds[r])
+
+        arrive_y(s - BLK)
+        arrive_z(s - BLK, fast)
+        apply(s, fast)
 
         @pl.when(s < ITERS * BLK)
         def _():
-            send(s)
-
-        products(s, v, (k * BLK - BLK, k * BLK))
+            send_z(s, fast)
+
+        products(s, v, others, (fast,))
+        arrive_z(s - BLK, core)
+        apply(s, core)
+
+        @pl.when(s < ITERS * BLK)
+        def _():
+            send_z(s, core)
+            send_y(s)
+
+        products(s, v, others, (core,), True)
         place(0, 2 * k - 1, v)
         place(1, 2 * k, v)
-
         split(k - 1, v)
-
-    pl.semaphore_wait(ready, (n_z - 1) + (Y_CHIPS - 1))
 
     def copy(stage, i):
         partner, _, me, base = stage
@@ -351,6 +385,7 @@
         for i in range(1, size):
             total = total + gathered[base + i]
 
+    sum_ref[...] = total
     weights = weights_of(total)
     eighth, within = lax.div(lanes, 8), lax.rem(lanes, 8)
     for i in range(0, BLK, 2):
@@ -373,16 +408,15 @@
             low = (both - high.astype(jnp.float32)).astype(jnp.bfloat16)
             mix_ref[8 * i : 8 * i + 16, start:stop] = high[:, : stop - start]
             mix_ref[64 + 8 * i : 64 + 8 * i + 16, start:stop] = low[:, : stop - start]
-    for h, tile in enumerate(hessenberg_of(total)):
-        hess_ref[8 * h : 8 * h + 8, :] = tile[:, : hess_ref.shape[1]]
-
     @pl.loop(0, ITERS * BLK)
     def _(s):
+        z_copy(s, fast).wait_send()
+
+        @pl.when(off_chip)
+        def _():
+            z_copy(s, core).wait_send()
+
         for up in (0, 1):
-
-            @pl.when(has_z[up])
-            def _(up=up):
-                z_copy(s, up).wait_send()
 
             @pl.when(has_y[up])
             def _(up=up):
@@ -393,14 +427,15 @@
             copy(stage, i).wait_send()
 
 
-def combine(high_ref, low_ref, mix_ref, h_ref, out_ref, hess_ref, result, out_sem):
-    hess_ref[...] = h_ref[...]
+def combine(high_ref, low_ref, mix_ref, sum_ref, out_ref, hess_ref, result, hess, out_sem, hess_sem):
     tiles = high_ref.shape[0] // 2
 
     def store(n):
         where = (slice(None), n // tiles, pl.ds(8 * (n % tiles), 8))
         return pltpu.make_async_copy(result.at[where], out_ref.at[where], out_sem.at[n])
 
+    for h, tile in enumerate(hessenberg_of(sum_ref[...])):
+        hess[8 * h : 8 * h + 8, :] = tile[:, : hess.shape[1]]
     for n in range(2 * tiles):
         both = jnp.dot(mix_ref[...], high_ref[n], preferred_element_type=jnp.float32)
         rest = jnp.dot(mix_ref[:64], low_ref[n], preferred_element_type=jnp.float32)
@@ -409,8 +444,11 @@
             BLK, 8, total.shape[1]
         )
         store(n).start()
+    copy = pltpu.make_async_copy(hess, hess_ref, hess_sem)
+    copy.start()
     for n in range(2 * tiles):
         store(n).wait()
+    copy.wait()
 
 
 def solution(mesh):
@@ -425,13 +463,13 @@
         vmem = lambda *shape: pltpu.VMEM(shape, jnp.float32)
         dma = pltpu.SemaphoreType.DMA
         whole = pl.BlockSpec(memory_space=pltpu.VMEM)
-        high, low, mix, hessenberg = pl.pallas_call(
+        high, low, mix, moments = pl.pallas_call(
             functools.partial(kernel, n_gz, n_gy),
             out_shape=(
                 jax.ShapeDtypeStruct((pieces, 8 * powers, n_cols), jnp.bfloat16),
                 jax.ShapeDtypeStruct((pieces, 8 * powers, n_cols), jnp.bfloat16),
                 jax.ShapeDtypeStruct((16 * BLK, 8 * powers), jnp.bfloat16),
-                jax.ShapeDtypeStruct((powers, powers + BLK), jnp.float32),
+                jax.ShapeDtypeStruct((8, 128), jnp.float32),
             ),
             in_specs=[pl.BlockSpec(memory_space=pltpu.HBM)] * 2,
             out_specs=(whole,) * 4,
@@ -452,7 +490,7 @@
                 dma((powers, 2)),
                 dma((partners,)),
                 dma((partners,)),
-                pltpu.SemaphoreType.REGULAR,
+                pltpu.SemaphoreType.REGULAR((16,)),
             ],
             compiler_params=pltpu.CompilerParams(
                 collective_id=0, has_side_effects=True, vmem_limit_bytes=28 << 20
@@ -463,14 +501,19 @@
             combine,
             out_shape=(
                 jax.ShapeDtypeStruct(right_side.shape, jnp.float32),
-                jax.ShapeDtypeStruct(hessenberg.shape, jnp.float32),
+                jax.ShapeDtypeStruct((powers, powers + BLK), jnp.float32),
             ),
             in_specs=[whole] * 4,
-            out_specs=(pl.BlockSpec(memory_space=pltpu.HBM), whole),
-            scratch_shapes=[vmem(*right_side.shape), dma((pieces,))],
+            out_specs=(pl.BlockSpec(memory_space=pltpu.HBM),) * 2,
+            scratch_shapes=[
+                vmem(*right_side.shape),
+                vmem(powers, powers + BLK),
+                dma((pieces,)),
+                dma,
+            ],
             compiler_params=pltpu.CompilerParams(vmem_limit_bytes=12 << 20),
             name="combine",
-        )(high, low, mix, hessenberg)
+        )(high, low, mix, moments)
 
     placed = (P(None, "gz", "gy", None), P("gz", "gy", None))
     return jax.shard_map(

time: 59.8 us -> 58.1 us (0.972)
  Pallas kernels: 59.1 us -> 57.3 us
    pallas_call x1, Pallas kernels: 56.4 us -> 55.2 us  [body(): pl.pallas_call(functools.partial(kernel, n_gz, n_gy), out_shape=(jax.Shap...]
where the time goes in v2:
time: 58.1 us; the launch traced here: 57.9 us
  Pallas kernels  57.3 us (99%)
  between operations  0.64 us (1%)
    pallas_call x1, Pallas kernels, body(): pl.pallas_call(functools.partial(kernel, n_gz, n_gy), out_shape=(jax.Shap...  55.2 us
    pallas_call x1, Pallas kernels, body(): pl.pallas_call(combine, out_shape=(jax.ShapeDtypeStruct(right_side.shape,...  2.14 us

profile of v2, /device:TPU:1, one launch (start us, length us, event | category | flops | bytes accessed | tf_op | source)
XLA Modules:
  0.0 57.9 jit_solution(10243039690227157548)
XLA Ops:
  0.6 55.2 %block_gmres.1 = (bf16[16,192,512]{2,1,0:T(8,128)(2,1)S(1)}, bf16[16,192,512]{2,1,0:T(8,128)(2,1)S(1)}, bf16[128,192]{1,0:T(8,128)(2,1)S(1)}, f32[8,128]{1,0:T(8,128)S(1)}) custom-call(f32[8,2,64,512]{3,2,1,0:T(8,128)} %b_ref.1, f32[2,64,512]{2,1,0:T(8,128)} %d_ref.1), custom_call_target="tpu_custom_call" | custom-call | tf_op jit(solution)/shard_map/block_gmres/pallas_call | solution.py:466
  55.8 2.1 %combine.1 = (f32[8,2,64,512]{3,2,1,0:T(8,128)}, f32[24,32]{1,0:T(8,128)}) custom-call(bf16[16,192,512]{2,1,0:T(8,128)(2,1)S(1)} %get-tuple-element.6.high_ref, bf16[16,192,512]{2,1,0:T(8,128)(2,1)S(1)} %get-tuple-element.7.low_ref, bf16[128,192]{1,0:T(8,128)(2,1)S(1)} %get-tuple-element.8.mix_ref, f32[8,128]{1,0:T(8,128)S(1)} %get-tuple-element.9.sum_ref), custom_call_target="tpu_custom_call" | custom-call | tf_op jit(solution)/shard_map/combine/pallas_call | solution.py:500

commit v3 on v2

--- a/solution.py
+++ b/solution.py
@@ -96,8 +96,8 @@
 
 def kernel(
     n_gz, n_gy, b_ref, d_ref, high_ref, low_ref, mix_ref, sum_ref,
-    field, low_high, side_in, side_out, diag, rows_of, moments, gathered,
-    load_sem, diag_sem, z_send, z_recv, y_send, y_recv, all_send, all_recv, ready,
+    field, low_high, side_in, side_out, diag, rows_of, moments, gathered, last,
+    load_sem, diag_sem, z_send, z_recv, y_send, y_recv, all_send, all_recv, ready, last_send, last_recv,
 ):
     gz, gy = lax.axis_index("gz"), lax.axis_index("gy")
     n_rows, n_cols = d_ref.shape[1], d_ref.shape[2]
@@ -327,10 +327,34 @@
     diag_copy.wait()
     diag[...] = diag[...] + (6.0 - SHIFT)
 
-    @pl.loop(BLK, (ITERS + 1) * BLK)
+    end = (ITERS + 1) * BLK - 1
+
+    def advance(s, k, v):
+        others = (k * BLK - BLK, k * BLK)
+        arrive_y(s - BLK)
+        arrive_z(s - BLK, fast)
+        apply(s, fast)
+        if s is not end:
+
+            @pl.when(s < ITERS * BLK)
+            def _():
+                send_z(s, fast)
+
+        products(s, v, others, (fast,))
+        arrive_z(s - BLK, core)
+        apply(s, core)
+        if s is not end:
+
+            @pl.when(s < ITERS * BLK)
+            def _():
+                send_z(s, core)
+                send_y(s)
+
+        products(s, v, others, (core,), True)
+
+    @pl.loop(BLK, end)
     def _(s):
         k, v = lax.div(s, BLK), lax.rem(s, BLK)
-        others = (k * BLK - BLK, k * BLK)
         for r in range(len(rounds) + 1):
 
             @pl.when(s == BLK + r)
@@ -340,24 +364,7 @@
                 if r < len(rounds):
                     tell(ready.at[r], *rounds[r])
 
-        arrive_y(s - BLK)
-        arrive_z(s - BLK, fast)
-        apply(s, fast)
-
-        @pl.when(s < ITERS * BLK)
-        def _():
-            send_z(s, fast)
-
-        products(s, v, others, (fast,))
-        arrive_z(s - BLK, core)
-        apply(s, core)
-
-        @pl.when(s < ITERS * BLK)
-        def _():
-            send_z(s, core)
-            send_y(s)
-
-        products(s, v, others, (core,), True)
+        advance(s, k, v)
         place(0, 2 * k - 1, v)
         place(1, 2 * k, v)
         split(k - 1, v)
@@ -373,17 +380,92 @@
             device_id_type=MESH,
         )
 
-    total = moments[...]
-    for stage in stages:
+    def start(stage, total):
         _, size, me, base = stage
         gathered[base + me] = total
         for i in range(1, size):
             copy(stage, i).start()
+
+    def finish(stage):
+        _, size, me, base = stage
         for i in range(1, size):
             copy(stage, i).wait_recv()
         total = gathered[base]
         for i in range(1, size):
             total = total + gathered[base + i]
+        return total
+
+    split(ITERS - 1, BLK - 1)
+    start(stages[0], moments[...])
+    advance(end, ITERS, BLK - 1)
+
+    halves = [jnp.sum(rows_of[at], axis=1, keepdims=True) for at in (0, 1)]
+    row = jnp.where(lanes == sub, halves[0], 0.0) + jnp.where(lanes == 8 + sub, halves[1], 0.0)
+    here = gz * n_gy + gy
+    last[here] = jnp.sum(row, axis=0, keepdims=True)
+    zs = [around(z_at, i, n_z) * (CORES * Y_CHIPS) for i in range(n_z)]
+    ys = [around(y_at, i, Y_CHIPS) * CORES for i in range(Y_CHIPS)]
+    xs = [around(gy, i, n_gy) for i in range(n_gy)]
+    cores = [core, fast]
+    far = lambda i, size: min(i, size - i)
+    others = [
+        (-(far(a, n_z) + far(b, Y_CHIPS) + far(c, n_gy)), -d, a, b, c)
+        for a in range(n_z) for b in range(Y_CHIPS) for c in range(n_gy) for d in range(CORES)
+        if a + b + c + d
+    ]
+
+    def last_copy(source, device):
+        return pltpu.make_async_remote_copy(
+            src_ref=source,
+            dst_ref=source,
+            send_sem=last_send,
+            recv_sem=last_recv,
+            device_id=device,
+            device_id_type=MESH,
+        )
+
+    for _, d, a, b, c in sorted(others):
+        last_copy(last.at[here], (zs[a] + ys[b] + cores[-d], xs[c])).start()
+    start(stages[1], finish(stages[0]))
+
+    @pl.loop(0, ITERS * BLK)
+    def _(s):
+        z_copy(s, fast).wait_send()
+
+        @pl.when(off_chip)
+        def _():
+            z_copy(s, core).wait_send()
+
+        for up in (0, 1):
+
+            @pl.when(has_y[up])
+            def _(up=up):
+                y_copy(s, up).wait_send()
+
+    for stage in stages:
+        for i in range(1, stage[1]):
+            copy(stage, i).wait_send()
+    everyone = last_copy(last.at[pl.ds(0, len(others))], (gz, gy))
+    everyone.wait_send()
+    total = finish(stages[1])
+    everyone.wait_recv()
+    sums = [last[i] for i in range(8)]
+    for i in range(8, n_gz * n_gy):
+        sums[i % 8] = sums[i % 8] + last[i]
+    while len(sums) > 1:
+        sums = [a + b for a, b in zip(sums[::2], sums[1::2])]
+    final = jnp.broadcast_to(sums[0], (8, 128))
+    at = 8 * (2 * ITERS - 1)
+    total = total + jnp.where(
+        jnp.logical_and(sub == 7, jnp.logical_and(lanes >= at, lanes < at + 16)),
+        pltpu.roll(final, at, 1),
+        0.0,
+    )
+    for n in (0, 1):
+        column = jnp.sum(jnp.where(lanes == 8 * n + sub, final, 0.0), axis=1, keepdims=True)
+        total = total + jnp.where(
+            jnp.logical_and(sub < 7, lanes == at + 8 * n + 7), column, 0.0
+        )
 
     sum_ref[...] = total
     weights = weights_of(total)
@@ -408,23 +490,6 @@
             low = (both - high.astype(jnp.float32)).astype(jnp.bfloat16)
             mix_ref[8 * i : 8 * i + 16, start:stop] = high[:, : stop - start]
             mix_ref[64 + 8 * i : 64 + 8 * i + 16, start:stop] = low[:, : stop - start]
-    @pl.loop(0, ITERS * BLK)
-    def _(s):
-        z_copy(s, fast).wait_send()
-
-        @pl.when(off_chip)
-        def _():
-            z_copy(s, core).wait_send()
-
-        for up in (0, 1):
-
-            @pl.when(has_y[up])
-            def _(up=up):
-                y_copy(s, up).wait_send()
-
-    for stage in stages:
-        for i in range(1, stage[1]):
-            copy(stage, i).wait_send()
 
 
 def combine(high_ref, low_ref, mix_ref, sum_ref, out_ref, hess_ref, result, hess, out_sem, hess_sem):
@@ -482,6 +547,7 @@
                 vmem(2, 8, 128),
                 vmem(8, 128),
                 vmem(partners, 8, 128),
+                vmem(n_gz * n_gy, 1, 128),
                 dma((BLK,)),
                 dma,
                 dma((powers, 2)),
@@ -491,6 +557,8 @@
                 dma((partners,)),
                 dma((partners,)),
                 pltpu.SemaphoreType.REGULAR((16,)),
+                dma,
+                dma,
             ],
             compiler_params=pltpu.CompilerParams(
                 collective_id=0, has_side_effects=True, vmem_limit_bytes=28 << 20

time: 58.1 us -> 56.9 us (0.979)
  Pallas kernels: 57.3 us -> 56.1 us
    pallas_call x1, Pallas kernels: 55.2 us -> 54 us  [body(): pl.pallas_call(functools.partial(kernel, n_gz, n_gy), out_shape=(jax.Shap...]
where the time goes in v3:
time: 56.9 us; the launch traced here: 56.8 us
  Pallas kernels  56.1 us (99%)
  between operations  0.64 us (1%)
    pallas_call x1, Pallas kernels, body(): pl.pallas_call(functools.partial(kernel, n_gz, n_gy), out_shape=(jax.Shap...  54 us
    pallas_call x1, Pallas kernels, body(): pl.pallas_call(combine, out_shape=(jax.ShapeDtypeStruct(right_side.shape,...  2.14 us

profile of v3, /device:TPU:1, one launch (start us, length us, event | category | flops | bytes accessed | tf_op | source)
XLA Modules:
  0.0 56.8 jit_solution(1195371606994757511)
XLA Ops:
  0.6 54.0 %block_gmres.1 = (bf16[16,192,512]{2,1,0:T(8,128)(2,1)S(1)}, bf16[16,192,512]{2,1,0:T(8,128)(2,1)S(1)}, bf16[128,192]{1,0:T(8,128)(2,1)S(1)}, f32[8,128]{1,0:T(8,128)S(1)}) custom-call(f32[8,2,64,512]{3,2,1,0:T(8,128)} %b_ref.1, f32[2,64,512]{2,1,0:T(8,128)} %d_ref.1), custom_call_target="tpu_custom_call" | custom-call | tf_op jit(solution)/shard_map/block_gmres/pallas_call | solution.py:531
  54.6 2.1 %combine.1 = (f32[8,2,64,512]{3,2,1,0:T(8,128)}, f32[24,32]{1,0:T(8,128)}) custom-call(bf16[16,192,512]{2,1,0:T(8,128)(2,1)S(1)} %get-tuple-element.6.high_ref, bf16[16,192,512]{2,1,0:T(8,128)(2,1)S(1)} %get-tuple-element.7.low_ref, bf16[128,192]{1,0:T(8,128)(2,1)S(1)} %get-tuple-element.8.mix_ref, f32[8,128]{1,0:T(8,128)S(1)} %get-tuple-element.9.sum_ref), custom_call_target="tpu_custom_call" | custom-call | tf_op jit(solution)/shard_map/combine/pallas_call | solution.py:568

commit v4 on v3

--- a/solution.py
+++ b/solution.py
@@ -14,6 +14,7 @@
 TOP = 8
 Y_CHIPS = 4
 CORES = 2
+CHUNK = 4
 
 
 def iotas():
@@ -36,8 +37,23 @@
     return guess * (1.5 - 0.5 * value * guess * guess)
 
 
-def weights_of(moments):
+def eliminate(x, rows, start, stop):
     sub, _ = iotas()
+    for k in range(start, stop):
+        g, q = divmod(k, 8)
+        column = rows[k]
+        inverse = 1.0 / sublane(column[g], q)
+        pivot = sublane(x[g], q) * inverse
+        for h in range(ITERS):
+            x[h] = x[h] - column[h] * pivot
+        x[g] = jnp.where(sub == q, pivot, x[g])
+        for r in range(k + 1, len(rows)):
+            factor = sublane(column[r // 8], r % 8) * inverse
+            rows[r] = [rows[r][h] - factor * column[h] for h in range(ITERS)]
+            rows[r][g] = jnp.where(sub == q, factor, rows[r][g])
+
+
+def begin_weights(moments):
     one = pltpu.roll(moments, 128 - 8, 1)
     two = pltpu.roll(moments, 128 - 16, 1)
     squares = two + (2.0 * SHIFT) * one + (SHIFT * SHIFT) * moments
@@ -45,19 +61,16 @@
     x = [right if h == 0 else pltpu.roll(right, 128 - 8 * h, 1) for h in range(ITERS)]
     tiles = [[lane(squares, 8 * j + v) for v in range(8)] for j in range(2 * ITERS - 1)]
     rows = [[tiles[a + h][i] for h in range(ITERS)] for a in range(ITERS) for i in range(8)]
-    size = 8 * ITERS
-    for k in range(size):
-        g, q = divmod(k, 8)
-        column = rows[k]
-        inverse = 1.0 / sublane(column[g], q)
-        pivot = sublane(x[g], q) * inverse
-        for h in range(ITERS):
-            x[h] = x[h] - column[h] * pivot
-        x[g] = jnp.where(sub == q, pivot, x[g])
-        for r in range(k + 1, size):
-            factor = sublane(column[r // 8], r % 8) * inverse
-            rows[r] = [rows[r][h] - factor * column[h] for h in range(ITERS)]
-            rows[r][g] = jnp.where(sub == q, factor, rows[r][g])
+    eliminate(x, rows, 0, 8)
+    return x, rows
+
+
+def end_weights(x, rows, fifth, sixth):
+    for v in range(8):
+        rows[8 + v][2] = rows[8 + v][2] + fifth[v]
+        rows[16 + v][1] = rows[16 + v][1] + fifth[v]
+        rows[16 + v][2] = rows[16 + v][2] + (sixth[v] + (2.0 * SHIFT) * fifth[v])
+    eliminate(x, rows, 8, 8 * ITERS)
     return x
 
 
@@ -96,7 +109,7 @@
 
 def kernel(
     n_gz, n_gy, b_ref, d_ref, high_ref, low_ref, mix_ref, sum_ref,
-    field, low_high, side_in, side_out, diag, rows_of, moments, gathered, last,
+    field, low_high, side_in, side_out, diag, rows_of, moments, latest, gathered, last,
     load_sem, diag_sem, z_send, z_recv, y_send, y_recv, all_send, all_recv, ready, last_send, last_recv,
 ):
     gz, gy = lax.axis_index("gz"), lax.axis_index("gy")
@@ -110,6 +123,29 @@
     own = pl.ds(TOP, n_rows)
     sub, lanes = iotas()
 
+    def partners(gz_step, gy_step):
+        both = []
+        for sign in (-1, 1):
+            to_gz, to_gy = gz + sign * gz_step, gy + sign * gy_step
+            there = jnp.logical_and(
+                jnp.logical_and(to_gz >= 0, to_gz < n_gz), jnp.logical_and(to_gy >= 0, to_gy < n_gy)
+            )
+            both.append((there, (to_gz, to_gy)))
+        return sum(jnp.where(there, 1, 0) for there, _ in both), both
+
+    def tell(semaphore, gz_step, gy_step):
+        count, both = partners(gz_step, gy_step)
+        for there, device in both:
+
+            @pl.when(there)
+            def _(device=device):
+                pl.semaphore_signal(semaphore, inc=1, device_id=device, device_id_type=MESH)
+
+        return count
+
+    barrier = pltpu.get_barrier_semaphore()
+    expected = tell(barrier, 1, 0) + tell(barrier, 0, 1)
+
     def load(v):
         return pltpu.make_async_copy(b_ref.at[v], field.at[v, :, own, :], load_sem.at[v])
 
@@ -123,87 +159,71 @@
     def around(at, i, size):
         return at + i if i == 0 else jnp.where(at + i >= size, at + (i - size), at + i)
 
-    def first(i):
+    def over_yx(i):
         return (gz + (around(y_at, i // n_gy, Y_CHIPS) - y_at) * CORES, around(gy, i % n_gy, n_gy))
 
-    def second(i):
+    def over_zc(i):
         to = (around(z_at, i // CORES, n_z) - z_at) * CORES * Y_CHIPS
         return (gz + to + around(core, i % CORES, CORES) - core, gy)
 
     stages = (
-        (first, Y_CHIPS * n_gy, y_at * n_gy + gy, 0),
-        (second, n_z * CORES, z_at * CORES + core, Y_CHIPS * n_gy),
+        (over_zc, n_z * CORES, z_at * CORES + core, Y_CHIPS * n_gy),
+        (over_yx, Y_CHIPS * n_gy, y_at * n_gy + gy, 0),
     )
 
-    def tell(semaphore, gz_step, gy_step):
-        count = 0
-        for sign in (-1, 1):
-            to_gz, to_gy = gz + sign * gz_step, gy + sign * gy_step
-            there = jnp.logical_and(
-                jnp.logical_and(to_gz >= 0, to_gz < n_gz), jnp.logical_and(to_gy >= 0, to_gy < n_gy)
-            )
-
-            @pl.when(there)
-            def _(to_gz=to_gz, to_gy=to_gy):
-                pl.semaphore_signal(
-                    semaphore, inc=1, device_id=(to_gz, to_gy), device_id_type=MESH
-                )
-
-            count += jnp.where(there, 1, 0)
-        return count
-
-    barrier = pltpu.get_barrier_semaphore()
-    expected = tell(barrier, 1, 0) + tell(barrier, 0, 1)
-
-    def clear(where, buffer, side):
+    def clear(where, at):
         @pl.when(where)
         def _():
             @pl.loop(0, ITERS * BLK)
             def _(s):
-                buffer[s, side] = jnp.zeros(buffer.shape[2:], jnp.float32)
-
-    clear(gz == 0, low_high, 0)
-    clear(gz == n_gz - 1, low_high, 1)
-    clear(gy == 0, side_in, 0)
-    clear(gy == n_gy - 1, side_in, 1)
+                buffer = at(s)
+                buffer[...] = jnp.zeros(buffer.shape, jnp.float32)
+
+    for side, z_edge, y_edge in ((0, 0, 0), (1, n_gz - 1, n_gy - 1)):
+        clear(gz == z_edge, lambda s, side=side: low_high.at[s, side])
+        clear(gy == y_edge, lambda s, side=side: side_in.at[side, s])
     moments[...] = jnp.zeros((8, 128), jnp.float32)
+    latest[...] = jnp.zeros((8, 128), jnp.float32)
 
     off_chip = jnp.where(core == 0, gz > 0, gz < n_gz - 1)
 
     pl.semaphore_wait(barrier, expected)
 
-    rounds = []
-    step = 1
-    while step < n_gz:
-        rounds.append((step, 0))
-        step *= 2
-    rounds += [(0, 1)] * (n_gy - 1)
-
-    def knows(r):
-        gz_step, gy_step = rounds[r]
-        count = 0
-        for sign in (-1, 1):
-            to_gz, to_gy = gz + sign * gz_step, gy + sign * gy_step
-            there = jnp.logical_and(
-                jnp.logical_and(to_gz >= 0, to_gz < n_gz), jnp.logical_and(to_gy >= 0, to_gy < n_gy)
-            )
-            count += jnp.where(there, 1, 0)
-        pl.semaphore_wait(ready.at[r], count)
-
-    def z_copy(s, up):
+    doublings = (n_gz - 1).bit_length()
+    rounds = doublings + n_gy - 1
+
+    def reach(r):
+        gz_step = 1
+        for i in range(1, doublings):
+            gz_step = jnp.where(r == i, 2**i, gz_step)
+        along_gz = r < doublings
+        return jnp.where(along_gz, gz_step, 0), jnp.where(along_gz, 0, 1)
+
+    def z_copy(s, up, size):
         return pltpu.make_async_remote_copy(
-            src_ref=field.at[s, up, own, :],
-            dst_ref=low_high.at[s, 1 - up],
+            src_ref=field.at[pl.ds(s, size), up, own, :],
+            dst_ref=low_high.at[pl.ds(s, size), 1 - up],
             send_sem=z_send.at[s, up],
             recv_sem=z_recv.at[s, 1 - up],
             device_id=(gz + 2 * up - 1, gy),
             device_id_type=MESH,
         )
 
+    def by_chunk(s, at_end, do):
+        edge = CHUNK - 1 if at_end else 0
+        if isinstance(s, int):
+            if s < ITERS * BLK and s % CHUNK == edge:
+                do(s - edge)
+            return
+
+        @pl.when(jnp.logical_and(s < ITERS * BLK, lax.rem(s, CHUNK) == edge))
+        def _():
+            do(s - edge)
+
     def y_copy(s, up):
         return pltpu.make_async_remote_copy(
-            src_ref=side_out.at[s, up],
-            dst_ref=side_in.at[s, 1 - up],
+            src_ref=side_out.at[up, pl.ds(s, CHUNK)],
+            dst_ref=side_in.at[1 - up, pl.ds(s, CHUNK)],
             send_sem=y_send.at[s, up],
             recv_sem=y_recv.at[s, 1 - up],
             device_id=(gz, gy + 2 * up - 1),
@@ -212,55 +232,57 @@
 
     has_y = (gy > 0, gy < n_gy - 1)
 
-    def send_z(s, layer):
-        if layer is fast:
-            z_copy(s, fast).start()
-        else:
-
-            @pl.when(off_chip)
-            def _():
-                z_copy(s, core).start()
-
-    def send_y(s):
+    def send_slow(s):
+        @pl.when(off_chip)
+        def _():
+            z_copy(s, core, 1).start()
+
+    def send_fast(s):
         for layer in (0, 1):
-            side_out[s, 0, layer] = field[s, layer, TOP : TOP + 1, :]
-            side_out[s, 1, layer] = field[s, layer, TOP + n_rows - 1 : TOP + n_rows, :]
-        for up in (0, 1):
-
-            @pl.when(has_y[up])
-            def _(up=up):
-                y_copy(s, up).start()
-
-    def arrive_y(s):
-        for up in (0, 1):
-
-            @pl.when(has_y[up])
-            def _(up=up):
-                y_copy(s, 1 - up).wait_recv()
-
+            side_out[0, s, layer] = field[s, layer, TOP : TOP + 1, :]
+            side_out[1, s, layer] = field[s, layer, TOP + n_rows - 1 : TOP + n_rows, :]
+
+        def start(at):
+            z_copy(at, fast, CHUNK).start()
+            for up in (0, 1):
+
+                @pl.when(has_y[up])
+                def _(up=up):
+                    y_copy(at, up).start()
+
+        by_chunk(s, True, start)
+
+    def arrive_fast(s):
+        def wait(at):
+            z_copy(at, core, CHUNK).wait_recv()
+            for up in (0, 1):
+
+                @pl.when(has_y[up])
+                def _(up=up):
+                    y_copy(at, 1 - up).wait_recv()
+
+        by_chunk(s, False, wait)
         for layer in (0, 1):
-            field[s, layer, TOP - 1 : TOP, :] = side_in[s, 0, layer]
-            field[s, layer, TOP + n_rows : TOP + n_rows + 1, :] = side_in[s, 1, layer]
-
-    def arrive_z(s, layer):
-        if layer is fast:
-            z_copy(s, core).wait_recv()
-        else:
-
-            @pl.when(off_chip)
-            def _():
-                z_copy(s, fast).wait_recv()
+            field[s, layer, TOP - 1 : TOP, :] = side_in[0, s, layer]
+            field[s, layer, TOP + n_rows : TOP + n_rows + 1, :] = side_in[1, s, layer]
+
+    def arrive_slow(s):
+        @pl.when(off_chip)
+        def _():
+            z_copy(s, fast, 1).wait_recv()
 
     lane_of_row = lax.broadcasted_iota(jnp.int32, (8, n_cols), 1)
 
-    def apply(s, layer):
+    def apply(s, layer, ghost=True):
         f = s - BLK
         for t in range(tiles):
             low = TOP + 8 * t
             here = field[f, layer, low : low + 8, :]
             beside = field[f, layer, low - 1 : low + 7, :] + field[f, layer, low + 1 : low + 9, :]
             other = field[f, 1 - layer, low : low + 8, :]
-            beside = beside + (other + low_high[f, layer, 8 * t : 8 * t + 8, :])
+            if ghost:
+                other = other + low_high[f, layer, 8 * t : 8 * t + 8, :]
+            beside = beside + other
             left = jnp.where(lane_of_row == 0, 0.0, pltpu.roll(here, 1, 1))
             right = jnp.where(lane_of_row == n_cols - 1, 0.0, pltpu.roll(here, n_cols - 1, 1))
             field[s, layer, low : low + 8, :] = diag[layer, 8 * t : 8 * t + 8, :] * here - (
@@ -274,30 +296,60 @@
         return jnp.sum(total, axis=0, keepdims=True)
 
     def products(s, v, others, layers, more=False):
-        @pl.loop(0, v + 1)
-        def _(u):
-            totals = [jnp.zeros((8, n_cols), jnp.float32) for _ in others]
+        def block(u, size):
+            totals = [jnp.zeros((8, n_cols), jnp.float32) for _ in range(size * len(others))]
             for layer in layers:
                 for t in range(tiles):
                     low = TOP + 8 * t
                     here = field[s, layer, low : low + 8, :]
                     totals = [
-                        total + here * field[u + other, layer, low : low + 8, :]
-                        for total, other in zip(totals, others)
+                        total + here * field[u + n % size + others[n // size], layer, low : low + 8, :]
+                        for n, total in enumerate(totals)
                     ]
-            for at, total in enumerate(totals):
+            for n, total in enumerate(totals):
                 new = fold(total)
+                to = pl.ds(u + n % size, 1)
                 if more:
-                    new = new + rows_of[at, pl.ds(u, 1), :]
-                rows_of[at, pl.ds(u, 1), :] = new
-
-    def place(at, j, v):
-        values = jnp.sum(rows_of[at], axis=1, keepdims=True)
-        values = jnp.where(sub <= v, values, 0.0)
-        new = jnp.where(lanes == j * 8 + v, values, 0.0)
-        turned = jnp.where(jnp.logical_and(lanes == j * 8 + sub, sub < v), values, 0.0)
+                    new = new + rows_of[n // size, to, :]
+                rows_of[n // size, to, :] = new
+
+        pairs = lax.div(v + 1, 2)
+
+        @pl.loop(0, pairs)
+        def _(n):
+            block(2 * n, 2)
+
+        @pl.when(lax.rem(v, 2) == 0)
+        def _():
+            block(v, 1)
+
+    def place(which, v):
+        change = jnp.zeros((8, 128), jnp.float32)
+        turned = jnp.zeros((8, 128), jnp.float32)
+        for at, j in which:
+            values = jnp.sum(rows_of[at], axis=1, keepdims=True)
+            change = change + jnp.where(
+                jnp.logical_and(sub <= v, lanes == j * 8 + v), values, 0.0
+            )
+            turned = turned + jnp.where(
+                jnp.logical_and(lanes == j * 8 + sub, sub < v), values, 0.0
+            )
         turned = jnp.sum(turned, axis=0, keepdims=True)
-        moments[...] = moments[...] + (new + jnp.where(sub == v, turned, 0.0))
+        moments[...] = moments[...] + (change + jnp.where(sub == v, turned, 0.0))
+
+    def place_latest(v):
+        change = jnp.zeros((8, 128), jnp.float32)
+        for at in (0, 1):
+            values = jnp.sum(rows_of[at], axis=1, keepdims=True)
+            change = change + jnp.where(
+                jnp.logical_or(
+                    jnp.logical_and(sub <= v, lanes == 16 * sub + (8 * at + v)),
+                    jnp.logical_and(sub < v, lanes == 16 * v + 8 * at + sub),
+                ),
+                values,
+                0.0,
+            )
+        latest[...] = latest[...] + change
 
     def split(k, part):
         for layer in (0, 1):
@@ -315,59 +367,17 @@
     @pl.loop(0, BLK)
     def _(v):
         load(v).wait()
-        send_z(v, core)
-        send_z(v, fast)
-        send_y(v)
+
+        send_slow(v)
+        send_fast(v)
 
     @pl.loop(0, BLK)
     def _(v):
         products(v, v, (0,), (0, 1))
-        place(0, 0, v)
+        place([(0, 0)], v)
 
     diag_copy.wait()
     diag[...] = diag[...] + (6.0 - SHIFT)
-
-    end = (ITERS + 1) * BLK - 1
-
-    def advance(s, k, v):
-        others = (k * BLK - BLK, k * BLK)
-        arrive_y(s - BLK)
-        arrive_z(s - BLK, fast)
-        apply(s, fast)
-        if s is not end:
-
-            @pl.when(s < ITERS * BLK)
-            def _():
-                send_z(s, fast)
-
-        products(s, v, others, (fast,))
-        arrive_z(s - BLK, core)
-        apply(s, core)
-        if s is not end:
-
-            @pl.when(s < ITERS * BLK)
-            def _():
-                send_z(s, core)
-                send_y(s)
-
-        products(s, v, others, (core,), True)
-
-    @pl.loop(BLK, end)
-    def _(s):
-        k, v = lax.div(s, BLK), lax.rem(s, BLK)
-        for r in range(len(rounds) + 1):
-
-            @pl.when(s == BLK + r)
-            def _(r=r):
-                if r > 0:
-                    knows(r - 1)
-                if r < len(rounds):
-                    tell(ready.at[r], *rounds[r])
-
-        advance(s, k, v)
-        place(0, 2 * k - 1, v)
-        place(1, 2 * k, v)
-        split(k - 1, v)
 
     def copy(stage, i):
         partner, _, me, base = stage
@@ -395,14 +405,90 @@
             total = total + gathered[base + i]
         return total
 
-    split(ITERS - 1, BLK - 1)
-    start(stages[0], moments[...])
-    advance(end, ITERS, BLK - 1)
-
-    halves = [jnp.sum(rows_of[at], axis=1, keepdims=True) for at in (0, 1)]
-    row = jnp.where(lanes == sub, halves[0], 0.0) + jnp.where(lanes == 8 + sub, halves[1], 0.0)
+    end = (ITERS + 1) * BLK - 1
+
+    def advance(s, k, v):
+        others = (k * BLK - BLK, k * BLK)
+        arrive_fast(s - BLK)
+        apply(s, fast)
+        products(s, v, others, (fast,))
+        arrive_slow(s - BLK)
+        apply(s, core)
+
+        @pl.when(s < ITERS * BLK)
+        def _():
+            send_slow(s)
+            send_fast(s)
+
+        products(s, v, others, (core,), True)
+
+    def advance_last():
+        s, v = end, BLK - 1
+        others = (s - v - BLK, s - v)
+        arrive_fast(s - BLK)
+        apply(s, fast)
+        products(s, v, others, (fast,))
+        apply(s, core, ghost=False)
+        products(s, v, others, (core,), True)
+        arrive_slow(s - BLK)
+
+        def block(u, holds_last):
+            totals = [jnp.zeros((8, n_cols), jnp.float32) for _ in range(4)]
+            for t in range(tiles):
+                low = TOP + 8 * t
+                ghost = low_high[s - BLK, core, 8 * t : 8 * t + 8, :]
+                for n in range(4):
+                    field_of = field[u + n % 2 + others[n // 2], core, low : low + 8, :]
+                    if holds_last and n == 3:
+                        field_of = 2.0 * field_of - ghost
+                    totals[n] = totals[n] + ghost * field_of
+            for n, total in enumerate(totals):
+                to = pl.ds(u + n % 2, 1)
+                rows_of[n // 2, to, :] = rows_of[n // 2, to, :] - fold(total)
+
+        @pl.loop(0, BLK // 2 - 1)
+        def _(n):
+            block(2 * n, False)
+
+        block(BLK - 2, True)
+
+    @pl.loop(BLK, end)
+    def _(s):
+        k, v = lax.div(s, BLK), lax.rem(s, BLK)
+
+        @pl.when(s <= BLK + rounds)
+        def _():
+            r = s - BLK
+
+            @pl.when(r > 0)
+            def _():
+                pl.semaphore_wait(ready.at[r - 1], partners(*reach(r - 1))[0])
+
+            @pl.when(r < rounds)
+            def _():
+                tell(ready.at[r], *reach(r))
+
+        @pl.when(s == ITERS * BLK)
+        def _():
+            start(stages[0], moments[...])
+
+        advance(s, k, v)
+
+        @pl.when(k < ITERS)
+        def _():
+            place([(0, 2 * k - 1), (1, 2 * k)], v)
+
+        @pl.when(k == ITERS)
+        def _():
+            place_latest(v)
+
+        split(k - 1, v)
+
+    advance_last()
+    place_latest(BLK - 1)
+
     here = gz * n_gy + gy
-    last[here] = jnp.sum(row, axis=0, keepdims=True)
+    last[here] = jnp.sum(latest[...], axis=0, keepdims=True)
     zs = [around(z_at, i, n_z) * (CORES * Y_CHIPS) for i in range(n_z)]
     ys = [around(y_at, i, Y_CHIPS) * CORES for i in range(Y_CHIPS)]
     xs = [around(gy, i, n_gy) for i in range(n_gy)]
@@ -427,20 +513,22 @@
     for _, d, a, b, c in sorted(others):
         last_copy(last.at[here], (zs[a] + ys[b] + cores[-d], xs[c])).start()
     start(stages[1], finish(stages[0]))
+    split(ITERS - 1, BLK - 1)
 
     @pl.loop(0, ITERS * BLK)
     def _(s):
-        z_copy(s, fast).wait_send()
-
         @pl.when(off_chip)
         def _():
-            z_copy(s, core).wait_send()
-
+            z_copy(s, core, 1).wait_send()
+
+    @pl.loop(0, ITERS * BLK // CHUNK)
+    def _(n):
+        z_copy(n * CHUNK, fast, CHUNK).wait_send()
         for up in (0, 1):
 
             @pl.when(has_y[up])
             def _(up=up):
-                y_copy(s, up).wait_send()
+                y_copy(n * CHUNK, up).wait_send()
 
     for stage in stages:
         for i in range(1, stage[1]):
@@ -448,6 +536,7 @@
     everyone = last_copy(last.at[pl.ds(0, len(others))], (gz, gy))
     everyone.wait_send()
     total = finish(stages[1])
+    x, rows = begin_weights(total)
     everyone.wait_recv()
     sums = [last[i] for i in range(8)]
     for i in range(8, n_gz * n_gy):
@@ -455,20 +544,24 @@
     while len(sums) > 1:
         sums = [a + b for a, b in zip(sums[::2], sums[1::2])]
     final = jnp.broadcast_to(sums[0], (8, 128))
-    at = 8 * (2 * ITERS - 1)
-    total = total + jnp.where(
-        jnp.logical_and(sub == 7, jnp.logical_and(lanes >= at, lanes < at + 16)),
-        pltpu.roll(final, at, 1),
-        0.0,
-    )
-    for n in (0, 1):
-        column = jnp.sum(jnp.where(lanes == 8 * n + sub, final, 0.0), axis=1, keepdims=True)
-        total = total + jnp.where(
-            jnp.logical_and(sub < 7, lanes == at + 8 * n + 7), column, 0.0
-        )
+    tiles_of = [
+        [
+            jnp.broadcast_to(
+                jnp.sum(
+                    jnp.where(lanes == 16 * sub + (8 * at + v), final, 0.0), axis=1, keepdims=True
+                ),
+                (8, 128),
+            )
+            for v in range(BLK)
+        ]
+        for at in (0, 1)
+    ]
+    for at in (0, 1):
+        for v in range(BLK):
+            total = jnp.where(lanes == 8 * (2 * ITERS - 1 + at) + v, tiles_of[at][v], total)
 
     sum_ref[...] = total
-    weights = weights_of(total)
+    weights = end_weights(x, rows, *tiles_of)
     eighth, within = lax.div(lanes, 8), lax.rem(lanes, 8)
     for i in range(0, BLK, 2):
         wide = []
@@ -541,10 +634,11 @@
             scratch_shapes=[
                 vmem(powers + BLK, layers, n_rows + 2 * TOP, n_cols),
                 vmem(powers, 2, n_rows, n_cols),
-                vmem(powers, 2, layers, 1, n_cols),
-                vmem(powers, 2, layers, 1, n_cols),
+                vmem(2, powers, layers, 1, n_cols),
+                vmem(2, powers, layers, 1, n_cols),
                 vmem(layers, n_rows, n_cols),
                 vmem(2, 8, 128),
+                vmem(8, 128),
                 vmem(8, 128),
                 vmem(partners, 8, 128),
                 vmem(n_gz * n_gy, 1, 128),

time: 56.9 us -> 55.6 us (0.977)
  Pallas kernels: 56.1 us -> 54.8 us
    pallas_call x1, Pallas kernels: 54 us -> 52.7 us  [body(): pl.pallas_call(functools.partial(kernel, n_gz, n_gy), out_shape=(jax.Shap...]
where the time goes in v4:
time: 55.6 us; the launch traced here: 55.5 us
  Pallas kernels  54.8 us (99%)
  between operations  0.64 us (1%)
    pallas_call x1, Pallas kernels, body(): pl.pallas_call(functools.partial(kernel, n_gz, n_gy), out_shape=(jax.Shap...  52.7 us
    pallas_call x1, Pallas kernels, body(): pl.pallas_call(combine, out_shape=(jax.ShapeDtypeStruct(right_side.shape,...  2.14 us

profile of v4, /device:TPU:1, one launch (start us, length us, event | category | flops | bytes accessed | tf_op | source)
XLA Modules:
  0.0 55.5 jit_solution(1611519272203629172)
XLA Ops:
  0.6 52.7 %block_gmres.1 = (bf16[16,192,512]{2,1,0:T(8,128)(2,1)S(1)}, bf16[16,192,512]{2,1,0:T(8,128)(2,1)S(1)}, bf16[128,192]{1,0:T(8,128)(2,1)S(1)}, f32[8,128]{1,0:T(8,128)S(1)}) custom-call(f32[8,2,64,512]{3,2,1,0:T(8,128)} %b_ref.1, f32[2,64,512]{2,1,0:T(8,128)} %d_ref.1), custom_call_target="tpu_custom_call" | custom-call | tf_op jit(solution)/shard_map/block_gmres/pallas_call | solution.py:624
  53.3 2.1 %combine.1 = (f32[8,2,64,512]{3,2,1,0:T(8,128)}, f32[24,32]{1,0:T(8,128)}) custom-call(bf16[16,192,512]{2,1,0:T(8,128)(2,1)S(1)} %get-tuple-element.6.high_ref, bf16[16,192,512]{2,1,0:T(8,128)(2,1)S(1)} %get-tuple-element.7.low_ref, bf16[128,192]{1,0:T(8,128)(2,1)S(1)} %get-tuple-element.8.mix_ref, f32[8,128]{1,0:T(8,128)S(1)} %get-tuple-element.9.sum_ref), custom_call_target="tpu_custom_call" | custom-call | tf_op jit(solution)/shard_map/combine/pallas_call | solution.py:662

commit v5 on v4

--- a/solution.py
+++ b/solution.py
@@ -232,10 +232,28 @@
 
     has_y = (gy > 0, gy < n_gy - 1)
 
+    last_sent = ITERS * BLK - 1
+    half = n_rows // 2
+
+    def half_copy(part, up):
+        return pltpu.make_async_remote_copy(
+            src_ref=field.at[last_sent, up, pl.ds(TOP + part * half, half), :],
+            dst_ref=low_high.at[last_sent, 1 - up, pl.ds(part * half, half)],
+            send_sem=z_send.at[last_sent + part, up],
+            recv_sem=z_recv.at[last_sent + part, 1 - up],
+            device_id=(gz + 2 * up - 1, gy),
+            device_id_type=MESH,
+        )
+
     def send_slow(s):
-        @pl.when(off_chip)
+        @pl.when(jnp.logical_and(off_chip, s < last_sent))
         def _():
             z_copy(s, core, 1).start()
+
+        @pl.when(jnp.logical_and(off_chip, s == last_sent))
+        def _():
+            half_copy(0, core).start()
+            half_copy(1, core).start()
 
     def send_fast(s):
         for layer in (0, 1):
@@ -430,11 +448,10 @@
         products(s, v, others, (fast,))
         apply(s, core, ghost=False)
         products(s, v, others, (core,), True)
-        arrive_slow(s - BLK)
-
-        def block(u, holds_last):
+
+        def block(u, holds_last, part):
             totals = [jnp.zeros((8, n_cols), jnp.float32) for _ in range(4)]
-            for t in range(tiles):
+            for t in range(part * tiles // 2, (part + 1) * tiles // 2):
                 low = TOP + 8 * t
                 ghost = low_high[s - BLK, core, 8 * t : 8 * t + 8, :]
                 for n in range(4):
@@ -446,11 +463,17 @@
                 to = pl.ds(u + n % 2, 1)
                 rows_of[n // 2, to, :] = rows_of[n // 2, to, :] - fold(total)
 
-        @pl.loop(0, BLK // 2 - 1)
-        def _(n):
-            block(2 * n, False)
-
-        block(BLK - 2, True)
+        for part in (0, 1):
+
+            @pl.when(off_chip)
+            def _(part=part):
+                half_copy(part, fast).wait_recv()
+
+            @pl.loop(0, BLK // 2 - 1)
+            def _(n, part=part):
+                block(2 * n, False, part)
+
+            block(BLK - 2, True, part)
 
     @pl.loop(BLK, end)
     def _(s):
@@ -515,11 +538,16 @@
     start(stages[1], finish(stages[0]))
     split(ITERS - 1, BLK - 1)
 
-    @pl.loop(0, ITERS * BLK)
+    @pl.loop(0, ITERS * BLK - 1)
     def _(s):
         @pl.when(off_chip)
         def _():
             z_copy(s, core, 1).wait_send()
+
+    @pl.when(off_chip)
+    def _():
+        half_copy(0, core).wait_send()
+        half_copy(1, core).wait_send()
 
     @pl.loop(0, ITERS * BLK // CHUNK)
     def _(n):
@@ -644,8 +672,8 @@
                 vmem(n_gz * n_gy, 1, 128),
                 dma((BLK,)),
                 dma,
-                dma((powers, 2)),
-                dma((powers, 2)),
+                dma((powers + 1, 2)),
+                dma((powers + 1, 2)),
                 dma((powers, 2)),
                 dma((powers, 2)),
                 dma((partners,)),

time: 55.6 us -> 55.5 us (level)
  no operation moved by 1% of the time
where the time goes in v5:
time: 55.5 us; the launch traced here: 55.4 us
  Pallas kernels  54.8 us (99%)
  between operations  0.64 us (1%)
    pallas_call x1, Pallas kernels, body(): pl.pallas_call(functools.partial(kernel, n_gz, n_gy), out_shape=(jax.Shap...  52.7 us
    pallas_call x1, Pallas kernels, body(): pl.pallas_call(combine, out_shape=(jax.ShapeDtypeStruct(right_side.shape,...  2.14 us

profile of v5, /device:TPU:1, one launch (start us, length us, event | category | flops | bytes accessed | tf_op | source)
XLA Modules:
  0.0 55.4 jit_solution(14117728217838167499)
XLA Ops:
  0.6 52.7 %block_gmres.1 = (bf16[16,192,512]{2,1,0:T(8,128)(2,1)S(1)}, bf16[16,192,512]{2,1,0:T(8,128)(2,1)S(1)}, bf16[128,192]{1,0:T(8,128)(2,1)S(1)}, f32[8,128]{1,0:T(8,128)S(1)}) custom-call(f32[8,2,64,512]{3,2,1,0:T(8,128)} %b_ref.1, f32[2,64,512]{2,1,0:T(8,128)} %d_ref.1), custom_call_target="tpu_custom_call" | custom-call | tf_op jit(solution)/shard_map/block_gmres/pallas_call | solution.py:652
  53.3 2.1 %combine.1 = (f32[8,2,64,512]{3,2,1,0:T(8,128)}, f32[24,32]{1,0:T(8,128)}) custom-call(bf16[16,192,512]{2,1,0:T(8,128)(2,1)S(1)} %get-tuple-element.6.high_ref, bf16[16,192,512]{2,1,0:T(8,128)(2,1)S(1)} %get-tuple-element.7.low_ref, bf16[128,192]{1,0:T(8,128)(2,1)S(1)} %get-tuple-element.8.mix_ref, f32[8,128]{1,0:T(8,128)S(1)} %get-tuple-element.9.sum_ref), custom_call_target="tpu_custom_call" | custom-call | tf_op jit(solution)/shard_map/combine/pallas_call | solution.py:690

commit v6 on v4

--- a/solution.py
+++ b/solution.py
@@ -456,9 +456,9 @@
     def _(s):
         k, v = lax.div(s, BLK), lax.rem(s, BLK)
 
-        @pl.when(s <= BLK + rounds)
-        def _():
-            r = s - BLK
+        @pl.when(jnp.logical_and(s <= BLK + 2 * rounds, lax.rem(s - BLK, 2) == 0))
+        def _():
+            r = lax.div(s - BLK, 2)
 
             @pl.when(r > 0)
             def _():

time: 55.6 us -> 55.6 us (level)
  no operation moved by 1% of the time
where the time goes in v6:
time: 55.6 us; the launch traced here: 55.5 us
  Pallas kernels  54.8 us (99%)
  between operations  0.64 us (1%)
    pallas_call x1, Pallas kernels, body(): pl.pallas_call(functools.partial(kernel, n_gz, n_gy), out_shape=(jax.Shap...  52.7 us
    pallas_call x1, Pallas kernels, body(): pl.pallas_call(combine, out_shape=(jax.ShapeDtypeStruct(right_side.shape,...  2.14 us

profile of v6, /device:TPU:1, one launch (start us, length us, event | category | flops | bytes accessed | tf_op | source)
XLA Modules:
  0.0 55.5 jit_solution(8600205004538951173)
XLA Ops:
  0.6 52.7 %block_gmres.1 = (bf16[16,192,512]{2,1,0:T(8,128)(2,1)S(1)}, bf16[16,192,512]{2,1,0:T(8,128)(2,1)S(1)}, bf16[128,192]{1,0:T(8,128)(2,1)S(1)}, f32[8,128]{1,0:T(8,128)S(1)}) custom-call(f32[8,2,64,512]{3,2,1,0:T(8,128)} %b_ref.1, f32[2,64,512]{2,1,0:T(8,128)} %d_ref.1), custom_call_target="tpu_custom_call" | custom-call | tf_op jit(solution)/shard_map/block_gmres/pallas_call | solution.py:624
  53.3 2.1 %combine.1 = (f32[8,2,64,512]{3,2,1,0:T(8,128)}, f32[24,32]{1,0:T(8,128)}) custom-call(bf16[16,192,512]{2,1,0:T(8,128)(2,1)S(1)} %get-tuple-element.6.high_ref, bf16[16,192,512]{2,1,0:T(8,128)(2,1)S(1)} %get-tuple-element.7.low_ref, bf16[128,192]{1,0:T(8,128)(2,1)S(1)} %get-tuple-element.8.mix_ref, f32[8,128]{1,0:T(8,128)S(1)} %get-tuple-element.9.sum_ref), custom_call_target="tpu_custom_call" | custom-call | tf_op jit(solution)/shard_map/combine/pallas_call | solution.py:662
